TPU v7x, 256 devices: a 8x8x2 block of a 8x8x16 slice. The times are simulated.
256 devices in a mesh: groups: 2 (over z), ep: 16 (over x, core), tp: 8 (over y).
Axes of the slice: x: 8, y: 8, z: 2, core: 2. Of those that a mesh axis runs over, the one named last changes fastest.
The devices are a block of a 8x8x16 slice.
Arguments:
- tokens: bfloat16 [1024, 7168], P(('groups', 'ep')), parts along dimension 0, may hold values from -6 to 6
- w_gate: bfloat16 [16, 7168, 2048], P('ep', None, 'tp'), may hold values from -0.0625 to 0.0625
- w_up: bfloat16 [16, 7168, 2048], P('ep', None, 'tp'), may hold values from -0.0625 to 0.0625
- w_down: bfloat16 [16, 2048, 7168], P('ep', 'tp'), may hold values from -0.1875 to 0.1875
- router_logits: float32 [1024, 8], P(('groups', 'ep')), parts along dimension 0, may hold values from -6 to 6
- expert_ids: int32 [1024, 8], P(('groups', 'ep')), parts along dimension 0, may hold values from 0 to 15, all different within a row; in each aligned block of 32 rows (0 to 31, 32 to 63, ...) at most 24 rows name the same one
- draft_lengths: int32 [128], P(('groups', 'ep')), parts along dimension 0, may hold values from 7 to 8
- accept_mask: int32 [128, 8], P(('groups', 'ep')), parts along dimension 0, may hold values 0 or 1
Outputs:
- mixed: bfloat16 [1024, 7168], P(('groups', 'ep'), 'tp'), parts along dimension 0
- accepted: int32 [2], P('groups'), parts along dimension 0
There are 2 independent parts, one for each index of `groups`. A program takes and returns all parts, laid end to end along the dimension named above; an argument that names none is the same for every part. Nothing has to cross between parts.
Inputs may be any that keep to these rules, and one draw needn't show every extreme that they name: `expert_ids`: each row names 8 different experts. Among the rows of one ep index (aligned blocks of 32 rows) no expert is named by more than 24 rows, and in every draw some expert is named by exactly 24 rows of some block.
All inputs are finite; a program needn't handle non-finite values. No bound on the sum of `accept_mask` on one device may be relied on, other than what follows from the above.
Results may differ from a plain program's by a relative error of at most 0.017.
Values may be sent and summed in bfloat16 or wider, within the bound.
No kernel may reach another device: no remote copies, remote signals or barrier semaphores. Data moves between devices by JAX's collectives and lax.ppermute only.
A program may use at most 128 MiB of HBM per device.

v0:
```python
import jax
import jax.numpy as jnp
from jax import lax
from jax.sharding import PartitionSpec as P

DRAFT = 8
EXPERTS = 16
CAP = 24


def sent_to_all(array, axis):
    copies = jnp.broadcast_to(array, (lax.axis_size(axis), *array.shape))
    return lax.all_to_all(copies, axis, split_axis=0, concat_axis=0, tiled=True)


def of_everyone(array, axis):
    everything = sent_to_all(array, axis)
    return jnp.sum(everything, axis=0)


def per_device(tokens, w_gate, w_up, w_down, router_logits, expert_ids, draft_lengths, accept_mask):
    tok_rows = tokens.shape[0]
    width = tokens.shape[1]
    top = expert_ids.shape[1]
    tp_count = lax.axis_size("tp")
    slice_width = width // tp_count
    live = jnp.arange(DRAFT, dtype=jnp.int32)[None, :] < draft_lengths[:, None]
    live_rows = live.reshape(tok_rows)
    live_tokens = jnp.where(live_rows[:, None], tokens, jnp.zeros((), tokens.dtype))
    sig = jax.nn.sigmoid(router_logits)
    gates = 2.827 * sig / jnp.sum(sig, axis=1, keepdims=True)
    flat_ids = expert_ids.reshape(-1)
    onehot = (flat_ids[:, None] == jnp.arange(EXPERTS, dtype=jnp.int32)[None, :]).astype(jnp.int32)
    rank = jnp.cumsum(onehot, axis=0) - 1
    slot = jnp.sum(rank * onehot, axis=1)
    target = flat_ids * CAP + slot
    source = jnp.arange(tok_rows * top, dtype=jnp.int32) // top
    own_cols = lax.dynamic_slice_in_dim(
        live_tokens, lax.axis_index("tp") * slice_width, slice_width, 1
    )
    sendbuf = jnp.zeros((EXPERTS * CAP, slice_width), tokens.dtype).at[target].set(own_cols[source])
    received = lax.all_to_all(
        sendbuf.reshape(EXPERTS, CAP, slice_width), "ep", split_axis=0, concat_axis=1, tiled=True
    )
    piece = lax.all_gather(received, "tp", axis=2, tiled=True)
    gate_sum = jnp.einsum("emd,edf->emf", piece, w_gate, preferred_element_type=jnp.float32)
    up_sum = jnp.einsum("emd,edf->emf", piece, w_up, preferred_element_type=jnp.float32)
    hidden = (jax.nn.silu(gate_sum) * up_sum).astype(jnp.bfloat16)
    partial_value = jnp.einsum("emf,efd->emd", hidden, w_down, preferred_element_type=jnp.float32)
    expert_out = lax.psum_scatter(
        partial_value.astype(jnp.bfloat16), "tp", scatter_dimension=2, tiled=True
    )
    returned = lax.all_to_all(expert_out, "ep", split_axis=1, concat_axis=0, tiled=True)
    flat_back = returned.reshape(EXPERTS * CAP, returned.shape[2])
    picked = flat_back[target].reshape(tok_rows, top, returned.shape[2])
    mixed = jnp.sum(gates[:, :, None] * picked.astype(jnp.float32), axis=1).astype(jnp.bfloat16)
    passed = accept_mask * live.astype(jnp.int32)
    prefix = jnp.cumprod(passed, axis=1)
    local_count = jnp.sum(prefix)
    total = of_everyone(local_count, "ep")
    accepted = total.reshape(1)
    return (mixed, accepted)


def solution(mesh):
    placed = (
        P(("groups", "ep"), None),
        P("ep", None, "tp"),
        P("ep", None, "tp"),
        P("ep", "tp", None),
        P(("groups", "ep"), None),
        P(("groups", "ep"), None),
        P(("groups", "ep")),
        P(("groups", "ep"), None),
    )
    return jax.shard_map(
        per_device,
        mesh=mesh,
        in_specs=placed,
        out_specs=(P(("groups", "ep"), "tp"), P("groups")),
        check_vma=False,
    )
```

profile of v0, /device:TPU:513, one launch (start us, length us, event | category | flops | bytes accessed | tf_op | source)
XLA Modules:
  0.0 286.3 jit_solution(15594155464627464665)
XLA Ops:
  7.2 0.1 all-gather.2.cloned.1.call-start
  7.2 0.8 copy.36
  8.0 0.1 eq.29
  8.1 0.1 eq.25
  8.2 0.7 broadcast_multiply_fusion
  8.9 0.6 reduce-window.6
  9.5 0.2 slice_reduce_fusion
  9.7 0.1 copy.35
  9.8 0.1 mul.55
  9.9 0.7 iota_compare_fusion.2
  10.6 0.1 lt.48
  10.7 0.1 fusion.23
  10.8 0.9 dynamic-slice_select_fusion
  11.7 3.5 %scatter_custom_fusion = bf16[384,896]{1,0:T(8,128)(2,1)S(1)} fusion(s32[256]{0:T(256)S(1)} %bitcast.67, bf16[32,896]{1,0:T(8,128)(2,1)S(1)} %dynamic-slice_select_fusion, s32[1024]{0:T(1024)S(1)} %pad_clamp_fusion.1, bf16[]{:T(256)} %constant.43.clone.1), kind=kCustom, calls=%fused_computation.19 | custom fusion | bytes 688130 | tf_op jit(solution)/shard_map/scatter | solution.py:41
  15.2 44.7 %all_to_all.27 = bf16[16,24,896]{2,1,0:T(8,128)(2,1)} all-to-all(bf16[16,24,896]{2,1,0:T(8,128)(2,1)S(1)} %bitcast.66), channel_id=1, replica_groups=mesh['groups'=2,'ep'=16,'tp'=8] {'ep'}, dimensions={0} | all-to-all | bytes 1376256 | tf_op jit(solution)/shard_map/all_to_all | solution.py:42
  59.9 0.1 all-gather.2.cloned.1.call-update
  60.0 0.1 reduce-scatter.4.cloned.1.call-start
  60.1 66.0 %all-gather.2.cloned.1.call-done = bf16[1,384,7168]{2,1,0:T(8,128)(2,1)} async-done(((bf16[1,384,896]{2,1,0:T(8,128)(2,1)}), bf16[1,384,7168]{2,1,0:T(8,128)(2,1)}) %all-gather.2.cloned.1.call-update) | async-done | bytes 5505040 | tf_op jit(solution)/shard_map/all_gather | solution.py:45
  126.1 0.0 copy-start.4
  126.1 0.0 copy-start.5
  126.1 5.4 %fusion.3 = f32[384,256]{1,0:T(8,128)S(1)} fusion(bf16[1,384,7168]{2,1,0:T(8,128)(2,1)} %all-gather.2.cloned.1.call-done, bf16[1,7168,256]{2,1,0:T(8,128)(2,1)} %param.9), kind=kOutput, calls=%fused_computation.8 | convolution fusion | flops 1409286144 | bytes 9568256 | tf_op jit(solution)/shard_map/emd,edf->emf/dot_general | solution.py:46
  131.5 0.0 copy-done.4
  131.5 0.9 copy-done.5
  132.4 0.0 copy-start
  132.4 1.6 fusion.13
  134.0 0.4 copy-done
  134.4 4.0 %fusion = bf16[1,384,7168]{2,1,0:T(8,128)(2,1)} fusion(bf16[384,256]{1,0:T(8,128)(2,1)S(1)} %fusion.13, bf16[1,256,7168]{2,1,0:T(8,128)(2,1)S(1)} %copy-done), kind=kOutput, calls=%fused_computation.4 | convolution fusion | flops 1412038656 | bytes 9371648 | tf_op jit(solution)/shard_map/emf,efd->emd/dot_general | solution.py:49
  138.4 24.0 %copy.41 = bf16[1,384,7168]{1,0,2:T(2,128)(2,1)} copy(bf16[1,384,7168]{2,1,0:T(8,128)(2,1)} %fusion) | data formatting | bytes 11010048
  162.4 7.4 %copy.51 = bf16[7168,1,384]{2,0,1:T(8,128)(2,1)} copy(bf16[7168,1,384]{2,1,0:T(2,128)(2,1)} %bitcast.60) | data formatting | bytes 11010048
  169.8 0.0 copy-start.2
  169.8 0.0 copy-start.3
  169.8 0.1 reduce-scatter.4.cloned.1.call-update
  169.9 0.6 copy-done.2
  170.5 0.0 copy-done.3
  170.5 0.1 broadcast_select_fusion
  170.6 0.2 reduce_window.9
  170.8 0.6 reduce_sum.51
  171.4 1.2 broadcast_in_dim.29
  172.6 7.6 %all-to-all-start.2 = ((s32[16,1,1]{2,1,0:T(1,128)}), s32[16,1,1]{2,1,0:T(1,128)S(1)}, u32[]{:S(2)}, u32[]{:S(2)}) async-start(s32[16,1,1]{2,1,0:T(1,128)} %broadcast_in_dim.29), calls=%async_computation.2 | async-start | bytes 16384 | tf_op jit(solution)/shard_map/all_to_all | solution.py:13
  180.2 57.8 %reduce-scatter.4.cloned.1.call-done = bf16[896,384]{1,0:T(8,128)(2,1)} async-done(((bf16[7168,384]{1,0:T(8,128)(2,1)}), bf16[896,384]{1,0:T(8,128)(2,1)}) %reduce-scatter.4.cloned.1.call-update) | async-done | bytes 688144
  238.0 1.8 reshape_bitcast_fusion
  239.8 0.0 copy-start.1
  239.8 2.3 copy.39
  242.1 0.5 broadcast.160
  242.6 4.8 %reduce.3 = bf16[384,896]{1,0:T(8,128)(2,1)S(1)} reduce(bf16[384,1,896]{2,1,0:T(2,128)(2,1)S(1)} %bitcast.63, bf16[]{:T(256)} %broadcast.160), dimensions={1}, to_apply=%bitcast.54.reduce_sub_computation | reduce | bytes 1376258
  247.5 1.0 reshape.202
  248.5 0.0 all-to-all-done.2
  248.5 7.4 %all-to-all-start.1 = ((bf16[16,2,10752]{2,1,0:T(2,128)(2,1)}), bf16[16,2,10752]{2,1,0:T(2,128)(2,1)S(1)}, u32[]{:S(2)}, u32[]{:S(2)}) async-start(bf16[16,2,10752]{2,1,0:T(2,128)(2,1)} %reshape.202), calls=%async_computation.1 | async-start | bytes 1376256 | tf_op jit(solution)/shard_map/all_to_all | solution.py:53
  256.0 0.0 copy-done.1
  256.0 0.1 copy.34
  256.1 0.7 reduce_sum.52
  256.7 19.8 %all-to-all-done.1 = bf16[16,2,10752]{2,1,0:T(2,128)(2,1)S(1)} async-done(((bf16[16,2,10752]{2,1,0:T(2,128)(2,1)}), bf16[16,2,10752]{2,1,0:T(2,128)(2,1)S(1)}, u32[]{:S(2)}, u32[]{:S(2)}) %all-to-all-start.1) | async-done | bytes 688160 | tf_op jit(solution)/shard_map/all_to_all | solution.py:53
  276.6 0.6 reshape.203
  277.2 0.1 copy.52
  277.2 1.2 gather_fusion
  278.4 1.0 fusion.18
  (9 shorter events, 0.1 us)
Async XLA Ops:
  7.2 118.9 %all-gather.2.cloned.1.call-start = ((), (), s32[]{:S(2)}) async-start(), calls=%async_computation.4 | async-start | bytes 6193152 | tf_op jit(solution)/shard_map/all_gather | solution.py:45
  60.0 178.0 %reduce-scatter.4.cloned.1.call-start = ((), (), s32[]{:S(2)}) async-start(), calls=%async_computation.5 | async-start | bytes 6193152
  126.1 5.4 %copy-start.4 = (bf16[1,384,7168]{2,1,0:T(8,128)(2,1)S(1)}, bf16[1,384,7168]{2,1,0:T(8,128)(2,1)}, u32[]{:S(2)}) copy-start(bf16[1,384,7168]{2,1,0:T(8,128)(2,1)} %all-gather.2.cloned.1.call-done) | copy-start | bytes 16515076
  126.1 6.3 %copy-start.5 = (bf16[1,7168,256]{2,1,0:T(8,128)(2,1)S(1)}, bf16[1,7168,256]{2,1,0:T(8,128)(2,1)}, u32[]{:S(2)}) copy-start(bf16[1,7168,256]{2,1,0:T(8,128)(2,1)} %param.10) | copy-start | bytes 11010052
  132.4 2.0 copy-start
  169.8 0.7 copy-start.2
  169.8 0.7 copy-start.3
  172.6 75.9 %all-to-all-start.2 = ((s32[16,1,1]{2,1,0:T(1,128)}), s32[16,1,1]{2,1,0:T(1,128)S(1)}, u32[]{:S(2)}, u32[]{:S(2)}) async-start(s32[16,1,1]{2,1,0:T(1,128)} %broadcast_in_dim.29), calls=%async_computation.2 | async-start | bytes 16384 | tf_op jit(solution)/shard_map/all_to_all | solution.py:13
  239.8 16.2 %copy-start.1 = (f32[32,8]{0,1:T(8,128)S(1)}, f32[32,8]{0,1:T(8,128)}, u32[]{:S(2)}) copy-start(f32[32,8]{0,1:T(8,128)} %param.12) | copy-start | bytes 3076
  248.5 28.1 %all-to-all-start.1 = ((bf16[16,2,10752]{2,1,0:T(2,128)(2,1)}), bf16[16,2,10752]{2,1,0:T(2,128)(2,1)S(1)}, u32[]{:S(2)}, u32[]{:S(2)}) async-start(bf16[16,2,10752]{2,1,0:T(2,128)(2,1)} %reshape.202), calls=%async_computation.1 | async-start | bytes 1376256 | tf_op jit(solution)/shard_map/all_to_all | solution.py:53
Sparse Core Ops, SparseCore 0:
  60.1 65.8 all-gather.1
  170.0 67.9 reduce-scatter.3
where the time goes:
time: 288 us; the launch traced here: 286 us
  waiting for transfers between devices  144 us (50%)
  local copies, waits for them, and re-layouts  47.2 us (16%)
  blocking collectives  44.7 us (16%)
  starting transfers between devices  15.1 us (5%)
  between operations  14.2 us (5%)
  matrix products  10.9 us (4%)
  other arithmetic  10.4 us (4%)
    all_gather x1, waiting for transfers between devices, per_device(): piece = lax.all_gather(received, 'tp', axis=2, tiled=True)  66 us
    unnamed x3, waiting for transfers between devices  57.9 us
    all_to_all x1, blocking collectives, per_device(): lax.all_to_all(sendbuf.reshape(EXPERTS, CAP, slice_width), 'ep', split_ax...  44.7 us
    unnamed x20, local copies, waits for them, and re-layouts  38.2 us
    all_to_all x1, waiting for transfers between devices, per_device(): lax.all_to_all(expert_out, 'ep', split_axis=1, concat_axis=0, tiled=True)  19.8 us
    all_to_all x1, starting transfers between devices, sent_to_all(): return lax.all_to_all(copies, axis, split_axis=0, concat_axis=0, tiled=True)  7.55 us
    all_to_all x1, starting transfers between devices, per_device(): lax.all_to_all(expert_out, 'ep', split_axis=1, concat_axis=0, tiled=True)  7.44 us
  transfers between devices with their start and end apart: 4, of which 3 were waited for; matrix products, arithmetic and copies ran while one was open for 5% of the time, Pallas kernels for 0%

commit v1 on v0

--- a/solution.py
+++ b/solution.py
@@ -42,7 +42,7 @@
     received = lax.all_to_all(
         sendbuf.reshape(EXPERTS, CAP, slice_width), "ep", split_axis=0, concat_axis=1, tiled=True
     )
-    piece = lax.all_gather(received, "tp", axis=2, tiled=True)
+    piece = jnp.concatenate(lax.all_gather(received, "tp"), axis=2)
     gate_sum = jnp.einsum("emd,edf->emf", piece, w_gate, preferred_element_type=jnp.float32)
     up_sum = jnp.einsum("emd,edf->emf", piece, w_up, preferred_element_type=jnp.float32)
     hidden = (jax.nn.silu(gate_sum) * up_sum).astype(jnp.bfloat16)

time: 288 us -> 302 us (1.049)
  matrix products: 10.9 us -> 18.3 us
  local copies, waits for them, and re-layouts: 47.2 us -> 54 us
    dot_general x1, matrix products: 3.96 us -> 13 us  [per_device(): jnp.einsum('emf,efd->emd', hidden, w_down, preferred_element_type=jnp.flo...]
    all_gather x0 -> x1, local copies, waits for them, and re-layouts: none -> 8.27 us  [per_device(): piece = jnp.concatenate(lax.all_gather(received, 'tp'), axis=2)]
    unnamed x20 -> x14, local copies, waits for them, and re-layouts: 38.2 us -> 36.8 us
  transfers between devices with their start and end apart: 4 -> 4, of which waited for: 3 -> 3; matrix products, arithmetic and copies ran while one was open for 5% -> 4% of each run, Pallas kernels for 0% -> 0%
where the time goes in v1:
time: 302 us; the launch traced here: 300 us
  waiting for transfers between devices  144 us (48%)
  local copies, waits for them, and re-layouts  54 us (18%)
  blocking collectives  44.7 us (15%)
  matrix products  18.3 us (6%)
  starting transfers between devices  15.3 us (5%)
  between operations  14.2 us (5%)
  other arithmetic  10.4 us (3%)
    all_gather x1, waiting for transfers between devices, per_device(): piece = jnp.concatenate(lax.all_gather(received, 'tp'), axis=2)  65.8 us
    unnamed x3, waiting for transfers between devices  57.9 us
    all_to_all x1, blocking collectives, per_device(): lax.all_to_all(sendbuf.reshape(EXPERTS, CAP, slice_width), 'ep', split_ax...  44.7 us
    unnamed x14, local copies, waits for them, and re-layouts  36.8 us
    all_to_all x1, waiting for transfers between devices, per_device(): lax.all_to_all(expert_out, 'ep', split_axis=1, concat_axis=0, tiled=True)  19.8 us
    dot_general x1, matrix products, per_device(): jnp.einsum('emf,efd->emd', hidden, w_down, preferred_element_type=jnp.flo...  13 us
    all_gather x1, local copies, waits for them, and re-layouts, per_device(): piece = jnp.concatenate(lax.all_gather(received, 'tp'), axis=2)  8.27 us
    all_to_all x1, starting transfers between devices, sent_to_all(): return lax.all_to_all(copies, axis, split_axis=0, concat_axis=0, tiled=True)  7.55 us
  transfers between devices with their start and end apart: 4, of which 3 were waited for; matrix products, arithmetic and copies ran while one was open for 4% of the time, Pallas kernels for 0%

profile of v1, /device:TPU:513, one launch (start us, length us, event | category | flops | bytes accessed | tf_op | source)
XLA Modules:
  0.0 300.5 jit_solution(10468521131872918739)
XLA Ops:
  7.2 0.1 all-gather.2.cloned.1.call-start
  7.2 0.8 copy.45
  8.0 0.1 eq.29
  8.1 0.1 eq.25
  8.2 0.7 broadcast_multiply_fusion
  8.9 0.6 reduce-window.6
  9.5 0.2 slice_reduce_fusion
  9.7 0.1 copy.44
  9.8 0.1 mul.55
  9.9 0.7 iota_compare_fusion.2
  10.6 0.1 lt.48
  10.7 0.1 fusion.17
  10.8 0.9 dynamic-slice_select_fusion
  11.7 3.5 %scatter_custom_fusion = bf16[384,896]{1,0:T(8,128)(2,1)S(1)} fusion(s32[256]{0:T(256)S(1)} %bitcast.73, bf16[32,896]{1,0:T(8,128)(2,1)S(1)} %dynamic-slice_select_fusion, s32[1024]{0:T(1024)S(1)} %pad_clamp_fusion.1, bf16[]{:T(256)} %constant.43.clone.1), kind=kCustom, calls=%fused_computation.17 | custom fusion | bytes 688130 | tf_op jit(solution)/shard_map/scatter | solution.py:41
  15.2 44.7 %all_to_all.24 = bf16[16,24,896]{2,1,0:T(8,128)(2,1)} all-to-all(bf16[16,24,896]{2,1,0:T(8,128)(2,1)S(1)} %bitcast.72), channel_id=1, replica_groups=mesh['groups'=2,'ep'=16,'tp'=8] {'ep'}, dimensions={0} | all-to-all | bytes 1376256 | tf_op jit(solution)/shard_map/all_to_all | solution.py:42
  59.9 0.1 all-gather.2.cloned.1.call-update
  60.0 0.2 reduce-scatter.4.cloned.1.call-start
  60.3 65.8 %all-gather.2.cloned.1.call-done = bf16[8,1,384,896]{3,2,1,0:T(8,128)(2,1)} async-done(((bf16[1,1,384,896]{3,2,1,0:T(8,128)(2,1)}), bf16[8,1,384,896]{3,2,1,0:T(8,128)(2,1)}) %all-gather.2.cloned.1.call-update) | async-done | bytes 5505040 | tf_op jit(solution)/shard_map/all_gather | solution.py:45
  126.0 8.3 %copy.48 = bf16[8,1,384,896]{2,3,0,1:T(8,128)(2,1)} copy(bf16[8,1,384,896]{3,2,1,0:T(8,128)(2,1)} %all-gather.2.cloned.1.call-done) | data formatting | bytes 11010048 | tf_op jit(solution)/shard_map/all_gather | solution.py:45
  134.3 5.3 %fusion.4 = f32[384,256]{1,0:T(8,128)S(1)} fusion(bf16[384,7168]{0,1:T(8,128)(2,1)} %bitcast.64, bf16[1,7168,256]{2,1,0:T(8,128)(2,1)} %param.9), kind=kOutput, calls=%fused_computation.9 | convolution fusion | flops 1409286144 | bytes 9568256 | tf_op jit(solution)/shard_map/emd,edf->emf/dot_general | solution.py:46
  139.6 13.0 %fusion = bf16[1,384,7168]{2,1,0:T(8,128)(2,1)} fusion(bf16[1,256,7168]{2,1,0:T(8,128)(2,1)} %param.11, bf16[384,7168]{0,1:T(8,128)(2,1)} %bitcast.65, bf16[1,7168,256]{2,1,0:T(8,128)(2,1)} %param.10, f32[384,256]{1,0:T(8,128)S(1)} %fusion.4), kind=kOutput, calls=%fused_computation.4 | convolution fusion | flops 2821914624 | bytes 18743296 | tf_op jit(solution)/shard_map/emf,efd->emd/dot_general | solution.py:49
  152.6 24.0 %copy.51 = bf16[1,384,7168]{1,0,2:T(2,128)(2,1)} copy(bf16[1,384,7168]{2,1,0:T(8,128)(2,1)} %fusion) | data formatting | bytes 11010048
  176.6 7.4 %copy.61 = bf16[7168,1,384]{2,0,1:T(8,128)(2,1)} copy(bf16[7168,1,384]{2,1,0:T(2,128)(2,1)} %bitcast.66) | data formatting | bytes 11010048
  184.0 0.0 copy-start.1
  184.0 0.0 copy-start.2
  184.0 0.1 reduce-scatter.4.cloned.1.call-update
  184.1 0.6 copy-done.1
  184.7 0.0 copy-done.2
  184.7 0.1 broadcast_select_fusion
  184.8 0.2 reduce_window.9
  185.0 0.6 reduce_sum.51
  185.6 1.2 broadcast_in_dim.29
  186.8 7.6 %all-to-all-start.2 = ((s32[16,1,1]{2,1,0:T(1,128)}), s32[16,1,1]{2,1,0:T(1,128)S(1)}, u32[]{:S(2)}, u32[]{:S(2)}) async-start(s32[16,1,1]{2,1,0:T(1,128)} %broadcast_in_dim.29), calls=%async_computation.2 | async-start | bytes 16384 | tf_op jit(solution)/shard_map/all_to_all | solution.py:13
  194.4 57.8 %reduce-scatter.4.cloned.1.call-done = bf16[896,384]{1,0:T(8,128)(2,1)} async-done(((bf16[7168,384]{1,0:T(8,128)(2,1)}), bf16[896,384]{1,0:T(8,128)(2,1)}) %reduce-scatter.4.cloned.1.call-update) | async-done | bytes 688144
  252.2 1.8 reshape_bitcast_fusion
  254.0 0.0 copy-start
  254.0 2.3 copy.49
  256.3 0.5 broadcast.160
  256.8 4.8 %reduce.3 = bf16[384,896]{1,0:T(8,128)(2,1)S(1)} reduce(bf16[384,1,896]{2,1,0:T(2,128)(2,1)S(1)} %bitcast.69, bf16[]{:T(256)} %broadcast.160), dimensions={1}, to_apply=%bitcast.48.reduce_sub_computation | reduce | bytes 1376258
  261.7 1.0 reshape.210
  262.7 0.0 all-to-all-done.2
  262.7 7.4 %all-to-all-start.1 = ((bf16[16,2,10752]{2,1,0:T(2,128)(2,1)}), bf16[16,2,10752]{2,1,0:T(2,128)(2,1)S(1)}, u32[]{:S(2)}, u32[]{:S(2)}) async-start(bf16[16,2,10752]{2,1,0:T(2,128)(2,1)} %reshape.210), calls=%async_computation.1 | async-start | bytes 1376256 | tf_op jit(solution)/shard_map/all_to_all | solution.py:53
  270.1 0.0 copy-done
  270.2 0.1 copy.43
  270.3 0.7 reduce_sum.52
  270.9 19.8 %all-to-all-done.1 = bf16[16,2,10752]{2,1,0:T(2,128)(2,1)S(1)} async-done(((bf16[16,2,10752]{2,1,0:T(2,128)(2,1)}), bf16[16,2,10752]{2,1,0:T(2,128)(2,1)S(1)}, u32[]{:S(2)}, u32[]{:S(2)}) %all-to-all-start.1) | async-done | bytes 688160 | tf_op jit(solution)/shard_map/all_to_all | solution.py:53
  290.8 0.6 reshape.211
  291.3 0.1 copy.62
  291.4 1.2 gather_fusion
  292.6 1.0 fusion.12
  (9 shorter events, 0.1 us)
Async XLA Ops:
  7.2 118.9 %all-gather.2.cloned.1.call-start = ((), (), s32[]{:S(2)}) async-start(), calls=%async_computation.4 | async-start | bytes 6193152 | tf_op jit(solution)/shard_map/all_gather | solution.py:45
  60.0 192.2 %reduce-scatter.4.cloned.1.call-start = ((), (), s32[]{:S(2)}) async-start(), calls=%async_computation.5 | async-start | bytes 6193152
  184.0 0.7 copy-start.1
  184.0 0.7 copy-start.2
  186.8 75.9 %all-to-all-start.2 = ((s32[16,1,1]{2,1,0:T(1,128)}), s32[16,1,1]{2,1,0:T(1,128)S(1)}, u32[]{:S(2)}, u32[]{:S(2)}) async-start(s32[16,1,1]{2,1,0:T(1,128)} %broadcast_in_dim.29), calls=%async_computation.2 | async-start | bytes 16384 | tf_op jit(solution)/shard_map/all_to_all | solution.py:13
  254.0 16.2 %copy-start = (f32[32,8]{0,1:T(8,128)S(1)}, f32[32,8]{0,1:T(8,128)}, u32[]{:S(2)}) copy-start(f32[32,8]{0,1:T(8,128)} %param.12) | copy-start | bytes 3076
  262.7 28.1 %all-to-all-start.1 = ((bf16[16,2,10752]{2,1,0:T(2,128)(2,1)}), bf16[16,2,10752]{2,1,0:T(2,128)(2,1)S(1)}, u32[]{:S(2)}, u32[]{:S(2)}) async-start(bf16[16,2,10752]{2,1,0:T(2,128)(2,1)} %reshape.210), calls=%async_computation.1 | async-start | bytes 1376256 | tf_op jit(solution)/shard_map/all_to_all | solution.py:53
Sparse Core Ops, SparseCore 0:
  60.1 65.8 all-gather.1
  184.2 67.9 reduce-scatter.3
